TPU v7x, 32 devices: a whole 2x2x4 slice. The times are simulated.
32 devices in a mesh: dp: 4 (over y, x), tensor: 8 (over z, core).
Axes of the slice: x: 2, y: 2, z: 4, core: 2. Of those that a mesh axis runs over, the one named last changes fastest.
Arguments:
- saved_input: bfloat16 [512, 8192], P(('dp', 'tensor')), may hold values from -8 to 8
- keep_bits: int32 [512, 448], P(('dp', 'tensor')), may hold values from -2147483648 to 2147483646, as said below
- norm_gain: bfloat16 [8192], P('dp'), may hold values from 0.099609375 to 1.8984375
- gate_weight: bfloat16 [8192, 14336], P('dp', 'tensor'), may hold values from -0.0625 to 0.0625
- up_weight: bfloat16 [8192, 14336], P('dp', 'tensor'), may hold values from -0.0625 to 0.0625
- down_weight: bfloat16 [14336, 8192], P('tensor', 'dp'), may hold values from -0.046875 to 0.046875
Outputs:
- layer_out: bfloat16 [512, 8192], P('tensor', 'dp')
- row_check: float32 [512], P('tensor')
Inputs may be any that keep to these rules, and one draw needn't show every extreme that they name: `keep_bits`: bit k of word w of a token is the keep bit of hidden unit 32 w + k.
All inputs are finite; a program needn't handle non-finite values.
Results may differ from a plain program's by a relative error of at most 0.017.
Values may be sent and summed in bfloat16 or wider, within the bound.
A program may use at most 64 MiB of HBM per device.

v0:
```python
import jax
import jax.numpy as jnp
from jax import lax
from jax.sharding import PartitionSpec as P

D = 8192


def on_device(saved_input, keep_bits, norm_gain, gate_weight, up_weight, down_weight):
    tensor_width = lax.axis_size("tensor")
    dp_width = lax.axis_size("dp")
    unit_words = lax.all_to_all(keep_bits, "tensor", split_axis=1, concat_axis=0, tiled=True)
    shifts = jnp.arange(32, dtype=jnp.int32)
    keep_mask = jnp.bitwise_and(jnp.right_shift(unit_words[:, :, None], shifts[None, None, :]), 1)
    keep_mask = keep_mask.reshape(unit_words.shape[0], -1)
    keep_scale = 2.0 * keep_mask.astype(jnp.float32)
    width_units = gate_weight.shape[1]
    columns = lax.all_to_all(saved_input, "dp", split_axis=1, concat_axis=0, tiled=True)
    collected = lax.all_gather(columns, "tensor", axis=0, tiled=True)
    per_device = saved_input.shape[0]
    collected = collected.reshape(tensor_width, dp_width, per_device, collected.shape[1])
    collected = collected.transpose(1, 0, 2, 3).reshape(-1, collected.shape[3])
    widened = collected.astype(jnp.float32)
    squares = lax.psum(jnp.sum(widened * widened, axis=1), "dp")
    inv_rms = lax.rsqrt(squares / D + 1e-05)
    normed = (widened * inv_rms[:, None] * norm_gain.astype(jnp.float32)[None, :]).astype(
        jnp.bfloat16
    )
    gate_part = jnp.dot(normed, gate_weight, preferred_element_type=jnp.float32)
    up_part = jnp.dot(normed, up_weight, preferred_element_type=jnp.float32)
    projected = lax.psum_scatter(
        jnp.concatenate((gate_part, up_part), axis=1).astype(jnp.bfloat16),
        "dp",
        scatter_dimension=0,
        tiled=True,
    ).astype(jnp.float32)
    gate_sum = projected[:, :width_units]
    up_sum = projected[:, width_units:]
    hidden = (jax.nn.silu(gate_sum) * up_sum * keep_scale).astype(jnp.bfloat16)
    partial_value = jnp.dot(
        lax.all_gather(hidden, "dp", axis=0, tiled=True),
        down_weight,
        preferred_element_type=jnp.float32,
    )
    mlp_sum = lax.psum_scatter(
        partial_value.astype(jnp.bfloat16), "tensor", scatter_dimension=0, tiled=True
    ).astype(jnp.float32)
    out_rows = mlp_sum.shape[0]
    first_row = lax.axis_index("tensor") * out_rows
    residual = lax.dynamic_slice_in_dim(collected, first_row, out_rows, 0)
    layer_out = (residual.astype(jnp.float32) + mlp_sum).astype(jnp.bfloat16)
    widened_out = layer_out.astype(jnp.float32)
    row_check = lax.psum(jnp.sum(widened_out * widened_out, axis=1), "dp") / D
    return (layer_out, row_check)


def solution(mesh):
    placed = (
        P(("dp", "tensor"), None),
        P(("dp", "tensor"), None),
        P("dp"),
        P("dp", "tensor"),
        P("dp", "tensor"),
        P("tensor", "dp"),
    )
    return jax.shard_map(
        on_device,
        mesh=mesh,
        in_specs=placed,
        out_specs=(P("tensor", "dp"), P("tensor")),
        check_vma=False,
    )
```

profile of v0, /device:TPU:0, one launch (start us, length us, event | category | flops | bytes accessed | tf_op | source)
XLA Modules:
  0.0 222.7 jit_solution(6830503011668420196)
XLA Ops:
  7.2 0.0 all-gather.3.cloned.1.call-start
  7.2 1.0 copy.31
  8.2 10.8 %all_to_all.35 = bf16[16,4,2048]{2,0,1:T(8,128)(2,1)} all-to-all(bf16[16,4,2048]{2,0,1:T(8,128)(2,1)S(1)} %bitcast.30), channel_id=1, replica_groups=mesh['dp'=4,'tensor'=8] {'dp'}, dimensions={1} | all-to-all | bytes 524288 | tf_op jit(solution)/shard_map/all_to_all | solution.py:18
  19.0 0.0 all-gather.3.cloned.1.call-update
  19.0 0.0 reduce-scatter.3.cloned.1.call-start
  19.1 0.7 convert_element_type.40
  19.8 28.3 %all-gather.3.cloned.1.call-done = bf16[512,2048]{1,0:T(8,128)(2,1)} async-done(((bf16[64,2048]{1,0:T(8,128)(2,1)}), bf16[512,2048]{1,0:T(8,128)(2,1)}) %all-gather.3.cloned.1.call-update) | async-done | bytes 2097168 | tf_op jit(solution)/shard_map/all_gather | solution.py:19
  48.1 0.0 copy-start
  48.1 1.9 copy.23
  49.9 0.3 copy-done
  50.3 0.0 copy-start.1
  50.3 0.5 multiply_reduce_fusion
  50.8 0.1 reduce_sum.21
  50.8 9.8 %psum.14 = f32[512]{0:T(512)S(1)} all-reduce(f32[512]{0:T(512)S(1)} %reduce_sum.21), channel_id=1, replica_groups=mesh['dp'=4,'tensor'=8] {'dp'}, use_global_device_ids=true, to_apply=%region_1.0 | all-reduce | flops 512 | bytes 4096 | tf_op jit(solution)/shard_map/psum | solution.py:24
  60.7 7.1 %convolution_convert_fusion.2 = bf16[512,1792]{1,0:T(8,128)(2,1)S(1)} fusion(bf16[2048,1792]{1,0:T(8,128)(2,1)} %param.9, bf16[512,2048]{1,0:T(8,128)(2,1)S(1)} %bitcast.26, f32[2048]{0:T(1024)S(1)} %convert_element_type.40, f32[512]{0:T(512)S(1)} %add_rsqrt_fusion), kind=kOutput, calls=%fused_computation.5 | convolution fusion | flops 3763208192 | bytes 11282432 | tf_op jit(solution)/shard_map/dot_general | solution.py:29
  67.8 0.0 copy-done.1
  67.8 7.1 %convolution_convert_fusion.1 = bf16[512,1792]{1,0:T(8,128)(2,1)S(1)} fusion(bf16[2048,1792]{1,0:T(8,128)(2,1)} %param.10, bf16[512,2048]{1,0:T(8,128)(2,1)S(1)} %bitcast.27, f32[2048]{0:T(1024)S(1)} %convert_element_type.40, f32[512]{0:T(512)S(1)} %add_rsqrt_fusion), kind=kOutput, calls=%fused_computation.4 | convolution fusion | flops 3763208192 | bytes 11282432 | tf_op jit(solution)/shard_map/dot_general | solution.py:30
  74.9 2.1 pad_maximum_fusion
  77.1 0.0 copy-start.2
  77.1 0.0 reduce-scatter.3.cloned.1.call-update
  77.1 0.7 copy-done.2
  77.8 0.1 all_to_all.30
  77.9 0.7 reshape.26
  78.7 3.4 %all-to-all-start.1 = ((s32[8,1,896]{2,1,0:T(1,128)}), s32[8,1,896]{2,1,0:T(1,128)S(1)}, u32[]{:S(2)}, u32[]{:S(2)}) async-start(s32[8,1,896]{2,1,0:T(1,128)} %reshape.26), calls=%async_computation.2 | async-start | bytes 57344 | tf_op jit(solution)/shard_map/all_to_all | solution.py:12
  82.0 0.0 all-gather.5.cloned.1.call-start
  82.1 0.1 shift_right_arithmetic.26
  82.2 5.5 %all-to-all-done.1 = s32[8,1,896]{2,1,0:T(1,128)S(1)} async-done(((s32[8,1,896]{2,1,0:T(1,128)}), s32[8,1,896]{2,1,0:T(1,128)S(1)}, u32[]{:S(2)}, u32[]{:S(2)}) %all-to-all-start.1) | async-done | bytes 28704 | tf_op jit(solution)/shard_map/all_to_all | solution.py:12
  87.7 0.5 broadcast.10
  88.2 0.7 reduce.1
  88.9 0.1 reshape.27
  89.0 0.1 copy.26
  89.1 0.1 shift_right_arithmetic.23
  89.1 0.3 copy.27
  89.5 33.7 %reduce-scatter.3.cloned.1.call-done = bf16[128,3584]{1,0:T(8,128)(2,1)} async-done(((bf16[512,3584]{1,0:T(8,128)(2,1)}), bf16[128,3584]{1,0:T(8,128)(2,1)}) %reduce-scatter.3.cloned.1.call-update) | async-done | bytes 917520 | tf_op jit(solution)/shard_map/reduce_scatter | solution.py:31
  123.1 1.4 convert_element_type.42
  124.5 1.1 fusion.1
  125.6 0.0 all-gather.5.cloned.1.call-update
  125.6 0.0 reduce-scatter.5.cloned.1.call-start
  125.7 33.1 %all-gather.5.cloned.1.call-done = bf16[512,1792]{1,0:T(8,128)(2,1)} async-done(((bf16[128,1792]{1,0:T(8,128)(2,1)}), bf16[512,1792]{1,0:T(8,128)(2,1)}) %all-gather.5.cloned.1.call-update) | async-done | bytes 1835024 | tf_op jit(solution)/shard_map/all_gather | solution.py:41
  158.8 8.9 %convolution_convert_fusion = bf16[512,2048]{1,0:T(8,128)(2,1)} fusion(bf16[512,1792]{1,0:T(8,128)(2,1)} %all-gather.5.cloned.1.call-done, bf16[1792,2048]{1,0:T(8,128)(2,1)} %param.11), kind=kOutput, calls=%fused_computation.3 | convolution fusion | flops 3759144960 | bytes 11272192 | tf_op jit(solution)/shard_map/dot_general | solution.py:40
  167.7 0.0 reduce-scatter.5.cloned.1.call-update
  167.7 36.2 %reduce-scatter.5.cloned.1.call-done = bf16[64,2048]{1,0:T(8,128)(2,1)} async-done(((bf16[512,2048]{1,0:T(8,128)(2,1)}), bf16[64,2048]{1,0:T(8,128)(2,1)}) %reduce-scatter.5.cloned.1.call-update) | async-done | bytes 262160 | tf_op jit(solution)/shard_map/reduce_scatter | solution.py:45
  204.0 1.9 multiply_reduce_fusion.1
  205.9 9.8 %psum.15 = f32[64]{0:T(128)S(1)} all-reduce(f32[64]{0:T(128)S(1)} %get-tuple-element.2), channel_id=1, replica_groups=mesh['dp'=4,'tensor'=8] {'dp'}, use_global_device_ids=true, to_apply=%region_5.6 | all-reduce | flops 64 | bytes 512 | tf_op jit(solution)/shard_map/psum | solution.py:53
  215.7 0.5 broadcast_multiply_fusion
  (4 shorter events, 0.0 us)
Async XLA Ops:
  7.2 40.9 %all-gather.3.cloned.1.call-start = ((), (), s32[]{:S(2)}) async-start(), calls=%async_computation.4 | async-start | bytes 2359296 | tf_op jit(solution)/shard_map/all_gather | solution.py:19
  19.0 104.1 %reduce-scatter.3.cloned.1.call-start = ((), (), s32[]{:S(2)}) async-start(), calls=%async_computation.5 | async-start | bytes 4587520 | tf_op jit(solution)/shard_map/reduce_scatter | solution.py:31
  48.1 2.2 copy-start
  50.3 17.5 %copy-start.1 = (bf16[4,8,16,2048]{3,2,1,0:T(8,128)(2,1)}, bf16[4,8,16,2048]{3,2,1,0:T(8,128)(2,1)S(1)}, u32[]{:S(2)}) copy-start(bf16[4,8,16,2048]{3,2,1,0:T(8,128)(2,1)S(1)} %copy.23) | copy-start | bytes 6291460
  77.1 0.8 copy-start.2
  78.7 9.0 %all-to-all-start.1 = ((s32[8,1,896]{2,1,0:T(1,128)}), s32[8,1,896]{2,1,0:T(1,128)S(1)}, u32[]{:S(2)}, u32[]{:S(2)}) async-start(s32[8,1,896]{2,1,0:T(1,128)} %reshape.26), calls=%async_computation.2 | async-start | bytes 57344 | tf_op jit(solution)/shard_map/all_to_all | solution.py:12
  82.0 76.8 %all-gather.5.cloned.1.call-start = ((), (), s32[]{:S(2)}) async-start(), calls=%async_computation.6 | async-start | bytes 2293760 | tf_op jit(solution)/shard_map/all_gather | solution.py:41
  125.6 78.3 %reduce-scatter.5.cloned.1.call-start = ((), (), s32[]{:S(2)}) async-start(), calls=%async_computation.7 | async-start | bytes 2359296 | tf_op jit(solution)/shard_map/reduce_scatter | solution.py:45
Sparse Core Ops, SparseCore 0:
  19.1 28.8 all-gather.2
  77.2 45.8 reduce-scatter.2
  125.7 33.0 all-gather.4
  167.8 36.0 reduce-scatter.4
where the time goes:
time: 223 us
  waiting for transfers between devices  137 us (61%)
  blocking collectives  30.4 us (14%)
  matrix products  23.1 us (10%)
  between operations  13.9 us (6%)
  other arithmetic  8.92 us (4%)
  local copies, waits for them, and re-layouts  5.94 us (3%)
  starting transfers between devices  3.51 us (2%)
    reduce_scatter x1, waiting for transfers between devices, on_device(): lax.psum_scatter(partial_value.astype(jnp.bfloat16), 'tensor', scatter_di...  36.2 us
    reduce_scatter x1, waiting for transfers between devices, on_device(): lax.psum_scatter(jnp.concatenate((gate_part, up_part), axis=1).astype(jnp...  33.7 us
    all_gather x1, waiting for transfers between devices, on_device(): lax.all_gather(hidden, 'dp', axis=0, tiled=True)  33.1 us
    all_gather x1, waiting for transfers between devices, on_device(): collected = lax.all_gather(columns, 'tensor', axis=0, tiled=True)  28.3 us
    all_to_all x1, blocking collectives, on_device(): lax.all_to_all(saved_input, 'dp', split_axis=1, concat_axis=0, tiled=True)  10.8 us
    psum x1, blocking collectives, on_device(): squares = lax.psum(jnp.sum(widened * widened, axis=1), 'dp')  9.83 us
    psum x1, blocking collectives, on_device(): row_check = lax.psum(jnp.sum(widened_out * widened_out, axis=1), 'dp') / D  9.79 us
    dot_general x1, matrix products, on_device(): jnp.dot(lax.all_gather(hidden, 'dp', axis=0, tiled=True), down_weight, pr...  8.89 us
  transfers between devices with their start and end apart: 5, of which 5 were waited for; matrix products, arithmetic and copies ran while one was open for 1% of the time, Pallas kernels for 0%

commit v1 on v0

--- a/solution.py
+++ b/solution.py
@@ -16,7 +16,10 @@
     keep_scale = 2.0 * keep_mask.astype(jnp.float32)
     width_units = gate_weight.shape[1]
     columns = lax.all_to_all(saved_input, "dp", split_axis=1, concat_axis=0, tiled=True)
-    collected = lax.all_gather(columns, "tensor", axis=0, tiled=True)
+    peers = lax.axis_size("tensor")
+    blocks = jnp.stack([columns for _ in range(peers)])
+    blocks = lax.all_to_all(blocks, "tensor", split_axis=0, concat_axis=0)
+    collected = jnp.concatenate(blocks, axis=0)
     per_device = saved_input.shape[0]
     collected = collected.reshape(tensor_width, dp_width, per_device, collected.shape[1])
     collected = collected.transpose(1, 0, 2, 3).reshape(-1, collected.shape[3])

time: 223 us -> 249 us (1.12)
  waiting for transfers between devices: 137 us -> 158 us
  starting transfers between devices: 3.51 us -> 8.34 us
    all_to_all x0 -> x1, waiting for transfers between devices: none -> 49 us  [on_device(): blocks = lax.all_to_all(blocks, 'tensor', split_axis=0, concat_axis=0)]
    all_gather x1 -> x0, waiting for transfers between devices: 28.3 us -> none  [on_device(): collected = lax.all_gather(columns, 'tensor', axis=0, tiled=True)]
    all_to_all x0 -> x1, starting transfers between devices: none -> 4.88 us  [on_device(): blocks = lax.all_to_all(blocks, 'tensor', split_axis=0, concat_axis=0)]
where the time goes in v1:
time: 249 us; the launch traced here: 248 us
  waiting for transfers between devices  158 us (63%)
  blocking collectives  28.9 us (12%)
  matrix products  23.9 us (10%)
  between operations  13.9 us (6%)
  starting transfers between devices  8.34 us (3%)
  other arithmetic  8.24 us (3%)
  local copies, waits for them, and re-layouts  6.83 us (3%)
    all_to_all x1, waiting for transfers between devices, on_device(): blocks = lax.all_to_all(blocks, 'tensor', split_axis=0, concat_axis=0)  49 us
    reduce_scatter x1, waiting for transfers between devices, on_device(): lax.psum_scatter(partial_value.astype(jnp.bfloat16), 'tensor', scatter_di...  36.2 us
    reduce_scatter x1, waiting for transfers between devices, on_device(): lax.psum_scatter(jnp.concatenate((gate_part, up_part), axis=1).astype(jnp...  34 us
    all_gather x1, waiting for transfers between devices, on_device(): lax.all_gather(hidden, 'dp', axis=0, tiled=True)  33.1 us
    all_to_all x1, blocking collectives, on_device(): lax.all_to_all(saved_input, 'dp', split_axis=1, concat_axis=0, tiled=True)  10.7 us
    psum x1, blocking collectives, on_device(): row_check = lax.psum(jnp.sum(widened_out * widened_out, axis=1), 'dp') / D  9.79 us
    dot_general x1, matrix products, on_device(): jnp.dot(lax.all_gather(hidden, 'dp', axis=0, tiled=True), down_weight, pr...  8.89 us
    psum x1, blocking collectives, on_device(): squares = lax.psum(jnp.sum(widened * widened, axis=1), 'dp')  8.37 us
  transfers between devices with their start and end apart: 5, of which 5 were waited for; matrix products, arithmetic and copies ran while one was open for 1% of the time, Pallas kernels for 0%

profile of v1, /device:TPU:0, one launch (start us, length us, event | category | flops | bytes accessed | tf_op | source)
XLA Modules:
  0.0 247.9 jit_solution(18390814775954757363)
XLA Ops:
  7.2 1.0 copy.31
  8.1 0.0 copy-start.2
  8.1 10.7 %all_to_all.37 = bf16[16,4,2048]{2,0,1:T(8,128)(2,1)S(1)} all-to-all(bf16[16,4,2048]{2,0,1:T(8,128)(2,1)S(1)} %bitcast.30), channel_id=1, replica_groups=mesh['dp'=4,'tensor'=8] {'dp'}, dimensions={1} | all-to-all | bytes 524288 | tf_op jit(solution)/shard_map/all_to_all | solution.py:18
  18.9 1.6 stack.5
  20.5 4.9 %all-to-all-start.1 = ((bf16[8,64,2048]{2,1,0:T(8,128)(2,1)}), bf16[8,64,2048]{2,1,0:T(8,128)(2,1)S(1)}, u32[]{:S(2)}, u32[]{:S(2)}) async-start(bf16[8,64,2048]{2,1,0:T(8,128)(2,1)} %stack.5), calls=%async_computation.1 | async-start | bytes 4194304 | tf_op jit(solution)/shard_map/all_to_all | solution.py:21
  25.4 0.0 reduce-scatter.3.cloned.1.call-start
  25.4 0.0 copy-done.2
  25.4 49.0 %all-to-all-done.1 = bf16[8,64,2048]{2,1,0:T(8,128)(2,1)S(1)} async-done(((bf16[8,64,2048]{2,1,0:T(8,128)(2,1)}), bf16[8,64,2048]{2,1,0:T(8,128)(2,1)S(1)}, u32[]{:S(2)}, u32[]{:S(2)}) %all-to-all-start.1) | async-done | bytes 2097184 | tf_op jit(solution)/shard_map/all_to_all | solution.py:21
  74.4 1.5 copy.23
  75.9 0.5 multiply_reduce_fusion
  76.4 0.1 reduce_sum.21
  76.4 8.4 %psum.14 = f32[512]{0:T(512)S(1)} all-reduce(f32[512]{0:T(512)S(1)} %reduce_sum.21), channel_id=1, replica_groups=mesh['dp'=4,'tensor'=8] {'dp'}, use_global_device_ids=true, to_apply=%region_1.0 | all-reduce | flops 512 | bytes 4096 | tf_op jit(solution)/shard_map/psum | solution.py:27
  84.8 0.0 copy-start
  84.8 7.9 %convolution_convert_fusion.2 = bf16[512,1792]{1,0:T(8,128)(2,1)S(1)} fusion(bf16[2048,1792]{1,0:T(8,128)(2,1)} %param.9, bf16[512,2048]{1,0:T(8,128)(2,1)} %bitcast.26, f32[2048]{0:T(1024)S(1)} %convert_element_type.40, f32[512]{0:T(512)S(1)} %add_rsqrt_fusion), kind=kOutput, calls=%fused_computation.5 | convolution fusion | flops 3763208192 | bytes 11282432 | tf_op jit(solution)/shard_map/dot_general | solution.py:32
  92.7 0.0 copy-done
  92.7 7.1 %convolution_convert_fusion.1 = bf16[512,1792]{1,0:T(8,128)(2,1)S(1)} fusion(bf16[2048,1792]{1,0:T(8,128)(2,1)} %param.10, bf16[512,2048]{1,0:T(8,128)(2,1)S(1)} %bitcast.28, f32[2048]{0:T(1024)S(1)} %convert_element_type.40, f32[512]{0:T(512)S(1)} %add_rsqrt_fusion), kind=kOutput, calls=%fused_computation.4 | convolution fusion | flops 3763208192 | bytes 11282432 | tf_op jit(solution)/shard_map/dot_general | solution.py:33
  99.8 2.1 pad_maximum_fusion
  101.9 0.0 copy-start.1
  101.9 0.0 reduce-scatter.3.cloned.1.call-update
  102.0 0.7 copy-done.1
  102.7 0.1 all_to_all.31
  102.8 0.7 reshape.25
  103.5 3.3 %all-to-all-start.2 = ((s32[8,1,896]{2,1,0:T(1,128)}), s32[8,1,896]{2,1,0:T(1,128)S(1)}, u32[]{:S(2)}, u32[]{:S(2)}) async-start(s32[8,1,896]{2,1,0:T(1,128)} %reshape.25), calls=%async_computation.3 | async-start | bytes 57344 | tf_op jit(solution)/shard_map/all_to_all | solution.py:12
  106.9 0.0 all-gather.2.cloned.1.call-start
  107.0 0.1 shift_right_arithmetic.26
  107.0 5.5 %all-to-all-done.2 = s32[8,1,896]{2,1,0:T(1,128)S(1)} async-done(((s32[8,1,896]{2,1,0:T(1,128)}), s32[8,1,896]{2,1,0:T(1,128)S(1)}, u32[]{:S(2)}, u32[]{:S(2)}) %all-to-all-start.2) | async-done | bytes 28704 | tf_op jit(solution)/shard_map/all_to_all | solution.py:12
  112.5 0.5 broadcast.11
  113.1 0.7 reduce.1
  113.8 0.1 reshape.26
  113.9 0.1 copy.26
  113.9 0.1 shift_right_arithmetic.23
  114.0 0.3 copy.27
  114.3 34.0 %reduce-scatter.3.cloned.1.call-done = bf16[128,3584]{1,0:T(8,128)(2,1)} async-done(((bf16[512,3584]{1,0:T(8,128)(2,1)}), bf16[128,3584]{1,0:T(8,128)(2,1)}) %reduce-scatter.3.cloned.1.call-update) | async-done | bytes 917520 | tf_op jit(solution)/shard_map/reduce_scatter | solution.py:34
  148.3 1.4 convert_element_type.42
  149.7 1.1 fusion.1
  150.8 0.0 all-gather.2.cloned.1.call-update
  150.8 0.0 reduce-scatter.5.cloned.1.call-start
  150.9 33.1 %all-gather.2.cloned.1.call-done = bf16[512,1792]{1,0:T(8,128)(2,1)} async-done(((bf16[128,1792]{1,0:T(8,128)(2,1)}), bf16[512,1792]{1,0:T(8,128)(2,1)}) %all-gather.2.cloned.1.call-update) | async-done | bytes 1835024 | tf_op jit(solution)/shard_map/all_gather | solution.py:44
  184.0 8.9 %convolution_convert_fusion = bf16[512,2048]{1,0:T(8,128)(2,1)} fusion(bf16[512,1792]{1,0:T(8,128)(2,1)} %all-gather.2.cloned.1.call-done, bf16[1792,2048]{1,0:T(8,128)(2,1)} %param.11), kind=kOutput, calls=%fused_computation.3 | convolution fusion | flops 3759144960 | bytes 11272192 | tf_op jit(solution)/shard_map/dot_general | solution.py:43
  192.9 0.0 reduce-scatter.5.cloned.1.call-update
  192.9 36.2 %reduce-scatter.5.cloned.1.call-done = bf16[64,2048]{1,0:T(8,128)(2,1)} async-done(((bf16[512,2048]{1,0:T(8,128)(2,1)}), bf16[64,2048]{1,0:T(8,128)(2,1)}) %reduce-scatter.5.cloned.1.call-update) | async-done | bytes 262160 | tf_op jit(solution)/shard_map/reduce_scatter | solution.py:48
  229.2 1.9 multiply_reduce_fusion.1
  231.1 9.8 %psum.15 = f32[64]{0:T(128)S(1)} all-reduce(f32[64]{0:T(128)S(1)} %get-tuple-element.2), channel_id=1, replica_groups=mesh['dp'=4,'tensor'=8] {'dp'}, use_global_device_ids=true, to_apply=%region_5.6 | all-reduce | flops 64 | bytes 512 | tf_op jit(solution)/shard_map/psum | solution.py:56
  240.9 0.5 broadcast_multiply_fusion
  (5 shorter events, 0.0 us)
Async XLA Ops:
  8.1 17.3 %copy-start.2 = (bf16[2048]{0:T(1024)(128)(2,1)S(1)}, bf16[2048]{0:T(1024)(128)(2,1)}, u32[]{:S(2)}) copy-start(bf16[2048]{0:T(1024)(128)(2,1)} %param.8) | copy-start | bytes 12292
  20.5 53.9 %all-to-all-start.1 = ((bf16[8,64,2048]{2,1,0:T(8,128)(2,1)}), bf16[8,64,2048]{2,1,0:T(8,128)(2,1)S(1)}, u32[]{:S(2)}, u32[]{:S(2)}) async-start(bf16[8,64,2048]{2,1,0:T(8,128)(2,1)} %stack.5), calls=%async_computation.1 | async-start | bytes 4194304 | tf_op jit(solution)/shard_map/all_to_all | solution.py:21
  25.4 123.0 %reduce-scatter.3.cloned.1.call-start = ((), (), s32[]{:S(2)}) async-start(), calls=%async_computation.5 | async-start | bytes 4587520 | tf_op jit(solution)/shard_map/reduce_scatter | solution.py:34
  84.8 7.9 %copy-start = (bf16[4,8,16,2048]{3,2,1,0:T(8,128)(2,1)S(1)}, bf16[4,8,16,2048]{3,2,1,0:T(8,128)(2,1)}, u32[]{:S(2)}) copy-start(bf16[4,8,16,2048]{3,2,1,0:T(8,128)(2,1)} %copy.23) | copy-start | bytes 6291460
  101.9 0.8 copy-start.1
  103.5 9.0 %all-to-all-start.2 = ((s32[8,1,896]{2,1,0:T(1,128)}), s32[8,1,896]{2,1,0:T(1,128)S(1)}, u32[]{:S(2)}, u32[]{:S(2)}) async-start(s32[8,1,896]{2,1,0:T(1,128)} %reshape.25), calls=%async_computation.3 | async-start | bytes 57344 | tf_op jit(solution)/shard_map/all_to_all | solution.py:12
  106.9 77.1 %all-gather.2.cloned.1.call-start = ((), (), s32[]{:S(2)}) async-start(), calls=%async_computation.6 | async-start | bytes 2293760 | tf_op jit(solution)/shard_map/all_gather | solution.py:44
  150.8 78.3 %reduce-scatter.5.cloned.1.call-start = ((), (), s32[]{:S(2)}) async-start(), calls=%async_computation.7 | async-start | bytes 2359296 | tf_op jit(solution)/shard_map/reduce_scatter | solution.py:48
Sparse Core Ops, SparseCore 0:
  102.1 46.1 reduce-scatter.2
  151.0 33.0 all-gather.1
  193.1 36.0 reduce-scatter.4
